TPU v7x, 32 devices: a whole 2x2x4 slice. The times are simulated.
32 devices in a mesh: seq: 8 (over z, x), res: 4 (over y, core).
Axes of the slice: x: 2, y: 2, z: 4, core: 2. Of those that a mesh axis runs over, the one named last changes fastest.
Arguments:
- alignment: bfloat16 [128, 4, 128, 256], P('seq', 'res'), may hold values from -8 to 8
- gain_attn: float32 [256], replicated, may hold values from 0.1 to 1.9
- w_proj: bfloat16 [256, 4, 256], replicated, may hold values from -0.75 to 0.75
- w_out: bfloat16 [256, 256], replicated, may hold values from -0.375 to 0.375
- gain_head: float32 [256], replicated, may hold values from 0.1 to 1.9
- w_head: bfloat16 [256, 23], replicated, may hold values from -1 to 1
- masked: int32 [128, 4, 128], P('res', None, 'seq'), may hold values from 0 to 1
- labels: int32 [128, 4, 128], P('res', None, 'seq'), may hold values from 0 to 22
Outputs:
- updated: bfloat16 [128, 4, 128, 256], P('res', None, 'seq')
- masked_loss: float32 [], replicated
- mask_share: float32 [], replicated
All inputs are finite; a program needn't handle non-finite values.
Results may differ from a plain program's by a relative error of at most 0.011.
Values may be sent and summed in bfloat16 or wider, within the bound.
A program may use at most 192 MiB of HBM per device.

v0:
```python
import jax
import jax.numpy as jnp
from jax import lax
from jax.sharding import PartitionSpec as P

HEADS = 8
HEAD_DIM = 32


def normalize(values, gain):
    mean = jnp.mean(values, axis=-1, keepdims=True)
    centred = values - mean
    spread = jnp.mean(centred * centred, axis=-1, keepdims=True)
    return centred * lax.rsqrt(spread + 1e-05) * gain


def project(flat_rows, gain_attn, w_proj):
    features = flat_rows.shape[1]
    normed = normalize(flat_rows.astype(jnp.float32), gain_attn).astype(jnp.bfloat16)
    return jnp.dot(
        normed, w_proj.reshape(features, 4 * features), preferred_element_type=jnp.float32
    ).astype(jnp.bfloat16)


def column_attention(queries, key_part, value_part):
    inv_root = HEAD_DIM ** (-0.5)
    scores = (
        jnp.einsum("shd,thd->hst", queries, key_part, preferred_element_type=jnp.float32) * inv_root
    )
    probs = jnp.exp(scores)
    totals = jnp.sum(probs, axis=2)
    weighted = jnp.einsum(
        "hst,thd->shd", probs.astype(jnp.bfloat16), value_part, preferred_element_type=jnp.float32
    )
    return (weighted, totals)


def finish(flat_rows, gated, w_out):
    summed = flat_rows.astype(jnp.float32) + jnp.dot(
        gated, w_out, preferred_element_type=jnp.float32
    )
    return summed.astype(jnp.bfloat16)


def on_device(alignment, gain_attn, w_proj, w_out, gain_head, w_head, masked, labels):
    weights = masked.reshape(-1).astype(jnp.float32)
    local_count = jnp.sum(weights)
    local_rows, single_block, segment, features = alignment.shape
    seq_devices = lax.axis_size("seq")
    split_view = alignment.reshape(local_rows, seq_devices, segment // seq_devices, features)
    column_block = lax.all_to_all(split_view, "seq", split_axis=1, concat_axis=0, tiled=True)
    seq_total, single, col_count, features = column_block.shape
    by_column = jnp.transpose(column_block.reshape(seq_total, col_count, features), (1, 0, 2))
    flat_rows = by_column.reshape(col_count * seq_total, features)
    projected = project(flat_rows, gain_attn, w_proj).reshape(
        col_count, seq_total, 4, HEADS, HEAD_DIM
    )

    def per_column(picked):
        weighted, totals = column_attention(picked[:, 0], picked[:, 1], picked[:, 2])
        attended = weighted / totals.T[:, :, None]
        gated_col = attended * jax.nn.sigmoid(picked[:, 3].astype(jnp.float32))
        return gated_col.reshape(seq_total, features).astype(jnp.bfloat16)

    gated = lax.map(per_column, projected).reshape(col_count * seq_total, features)
    result = finish(flat_rows, gated, w_out).reshape(col_count, seq_total, features)
    result = jnp.transpose(result, (1, 0, 2)).reshape(seq_total, single, col_count, features)
    updated = lax.all_to_all(result, "res", split_axis=0, concat_axis=1, tiled=True)
    features = updated.shape[3]
    flat_out = updated.reshape(-1, features)
    head_in = normalize(flat_out.astype(jnp.float32), gain_head).astype(jnp.bfloat16)
    logits = jnp.einsum("rc,ck->kr", head_in, w_head, preferred_element_type=jnp.float32)
    log_total = jnp.log(jnp.sum(jnp.exp(logits), axis=0))
    classes = jnp.arange(logits.shape[0], dtype=jnp.int32)[:, None]
    picked = jnp.sum(jnp.where(classes == labels.reshape(1, -1), logits, 0.0), axis=0)
    errors = log_total - picked
    local_loss = jnp.sum(errors * weights)
    loss_sum, mask_count = lax.psum((local_loss, local_count), ("seq", "res"))
    entries = flat_out.shape[0] * lax.axis_size("seq") * lax.axis_size("res")
    masked_loss = loss_sum / (1.0 + mask_count)
    mask_share = mask_count / entries
    return (updated, masked_loss, mask_share)


def solution(mesh):
    in_specs = (
        P("seq", "res", None, None),
        P(),
        P(),
        P(),
        P(),
        P(),
        P("res", None, "seq"),
        P("res", None, "seq"),
    )
    out_specs = (P("res", None, "seq", None), P(), P())
    return jax.shard_map(
        on_device, mesh=mesh, in_specs=in_specs, out_specs=out_specs, check_vma=False
    )
```

profile of v0, /device:TPU:12, one launch (start us, length us, event | category | flops | bytes accessed | tf_op | source)
XLA Modules:
  0.0 152.1 jit_solution(10787070603162363327)
XLA Ops:
  0.7 2.4 %copy.61 = bf16[16,8,16,256]{3,2,0,1:T(8,128)(2,1)} copy(bf16[16,8,16,256]{3,2,1,0:T(8,128)(2,1)} %bitcast.113) | data formatting | bytes 2097152 | tf_op jit(solution)/shard_map/reshape | solution.py:50
  3.0 6.3 %all-to-all-start = ((bf16[16,8,16,256]{3,2,0,1:T(8,128)(2,1)}), bf16[16,8,16,256]{3,2,0,1:T(8,128)(2,1)S(1)}, u32[]{:S(2)}, u32[]{:S(2)}) async-start(bf16[16,8,16,256]{3,2,0,1:T(8,128)(2,1)} %copy.61), calls=%async_computation | async-start | bytes 2097152 | tf_op jit(solution)/shard_map/all_to_all | solution.py:51
  9.4 23.3 %all-to-all-done = bf16[16,8,16,256]{3,2,0,1:T(8,128)(2,1)S(1)} async-done(((bf16[16,8,16,256]{3,2,0,1:T(8,128)(2,1)}), bf16[16,8,16,256]{3,2,0,1:T(8,128)(2,1)S(1)}, u32[]{:S(2)}, u32[]{:S(2)}) %all-to-all-start) | async-done | bytes 1048608 | tf_op jit(solution)/shard_map/all_to_all | solution.py:51
  32.9 1.2 bitcast_reduce_fusion
  34.1 1.2 copy.62
  35.3 1.6 %multiply_reduce_fusion.1 = f32[16,128]{1,0:T(8,128)S(1)} fusion(f32[16,128]{1,0:T(8,128)S(1)} %broadcast_multiply_fusion.1, f32[128,16,256]{2,1,0:T(8,128)S(1)} %bitcast.100), kind=kLoop, calls=%fused_computation.24 | loop fusion | flops 1570816 | bytes 2113536 | tf_op jit(solution)/shard_map/reduce_sum | solution.py:13
  37.0 1.4 multiply_convert_fusion
  38.3 3.2 %convolution_convert_fusion = bf16[2048,1024]{1,0:T(8,128)(2,1)} fusion(bf16[2048,256]{1,0:T(8,128)(2,1)S(1)} %bitcast.109, bf16[256,1024]{1,0:T(8,128)(2,1)S(1)} %bitcast.111), kind=kOutput, calls=%fused_computation.12 | convolution fusion | flops 1075838976 | bytes 5767168 | tf_op jit(solution)/shard_map/dot_general | solution.py:20
  41.5 6.5 %copy.63 = bf16[2048,1024]{0,1:T(8,128)(2,1)} copy(bf16[2048,1024]{1,0:T(8,128)(2,1)} %convolution_convert_fusion) | data formatting | bytes 8388608 | tf_op jit(solution)/shard_map/convert_element_type | solution.py:22
  48.0 3.6 %copy.80 = bf16[128,8,16,128]{3,2,1,0:T(8,128)(2,1)S(1)} copy(bf16[128,8,16,128]{3,1,2,0:T(8,128)(2,1)} %bitcast.106) | data formatting | bytes 8388608
  51.6 3.0 %copy.64 = bf16[16,128,4,8,32]{1,4,3,2,0:T(8,128)(2,1)} copy(bf16[16,128,4,8,32]{1,0,4,3,2:T(8,128)(2,1)S(1)} %bitcast.107) | data formatting | bytes 8388608 | tf_op jit(solution)/shard_map/while | solution.py:65
  54.7 26.1 %while.10 = (s32[]{:T(128)}, bf16[16,128,256]{2,1,0:T(8,128)(2,1)S(1)}, bf16[16,128,4,8,32]{1,4,3,2,0:T(8,128)(2,1)}, s32[]{:T(128)}) while((s32[]{:T(128)}, bf16[16,128,256]{2,1,0:T(8,128)(2,1)S(1)}, bf16[16,128,4,8,32]{1,4,3,2,0:T(8,128)(2,1)}, s32[]{:T(128)}) %tuple.42), condition=%wide.region_4.0_spmd, body=%wide.region_2.4_spmd.sunk | while | flops 17398784 | bytes 1646653 | solution.py:65
  56.3 1.0 dynamic-slice_bitcast_fusion.2
  57.9 1.0 dynamic-slice_bitcast_fusion.2
  59.6 1.0 dynamic-slice_bitcast_fusion.2
  61.2 1.0 dynamic-slice_bitcast_fusion.2
  62.8 1.0 dynamic-slice_bitcast_fusion.2
  64.5 1.0 dynamic-slice_bitcast_fusion.2
  66.1 1.0 dynamic-slice_bitcast_fusion.2
  67.7 1.0 dynamic-slice_bitcast_fusion.2
  69.4 1.0 dynamic-slice_bitcast_fusion.2
  71.0 1.0 dynamic-slice_bitcast_fusion.2
  72.6 1.0 dynamic-slice_bitcast_fusion.2
  74.3 1.0 dynamic-slice_bitcast_fusion.2
  75.9 1.0 dynamic-slice_bitcast_fusion.2
  77.5 1.0 dynamic-slice_bitcast_fusion.2
  81.3 1.6 %copy.85 = bf16[16,128,256]{2,0,1:T(8,128)(2,1)} copy(bf16[16,128,256]{2,1,0:T(8,128)(2,1)S(1)} %bitcast.110) | data formatting | bytes 2097152 | tf_op jit(solution)/shard_map/reshape | solution.py:66
  82.8 4.0 %all-to-all-start.1 = ((bf16[128,1,16,256]{3,2,1,0:T(8,128)(2,1)}), bf16[128,1,16,256]{3,2,1,0:T(8,128)(2,1)S(1)}, u32[]{:S(2)}, u32[]{:S(2)}) async-start(bf16[128,1,16,256]{3,2,1,0:T(8,128)(2,1)} %bitcast.79), calls=%async_computation.1 | async-start | bytes 2097152 | tf_op jit(solution)/shard_map/all_to_all | solution.py:68
  87.1 12.5 %all-to-all-done.1 = bf16[128,1,16,256]{3,2,1,0:T(8,128)(2,1)S(1)} async-done(((bf16[128,1,16,256]{3,2,1,0:T(8,128)(2,1)}), bf16[128,1,16,256]{3,2,1,0:T(8,128)(2,1)S(1)}, u32[]{:S(2)}, u32[]{:S(2)}) %all-to-all-start.1) | async-done | bytes 1048608 | tf_op jit(solution)/shard_map/all_to_all | solution.py:68
  102.5 1.1 exponential_reduce_fusion
  104.4 42.4 %all-reduce = (f32[]{:T(128)}, f32[]{:T(128)}) all-reduce(f32[]{:T(128)} %get-tuple-element.57, f32[]{:T(128)} %get-tuple-element.56), channel_id=1, replica_groups=mesh['seq'=8,'res'=4] {'seq','res'}, use_global_device_ids=true, to_apply=%region_10.11 | all-reduce | flops 2 | bytes 16 | tf_op jit(solution)/shard_map/psum | solution.py:78
  148.1 1.1 copy.75
  (105 shorter events, 16.6 us)
Async XLA Ops:
  0.6 80.2 %copy-start = (bf16[256,256]{1,0:T(8,128)(2,1)S(1)}, bf16[256,256]{1,0:T(8,128)(2,1)}, u32[]{:S(2)}) copy-start(bf16[256,256]{1,0:T(8,128)(2,1)} %param.13) | copy-start | bytes 393220
  0.6 8.6 %copy-start.2 = (bf16[256,4,256]{2,1,0:T(4,128)(2,1)S(1)}, bf16[256,4,256]{2,1,0:T(4,128)(2,1)}, u32[]{:S(2)}) copy-start(bf16[256,4,256]{2,1,0:T(4,128)(2,1)} %param.12) | copy-start | bytes 1572868
  3.0 29.6 %all-to-all-start = ((bf16[16,8,16,256]{3,2,0,1:T(8,128)(2,1)}), bf16[16,8,16,256]{3,2,0,1:T(8,128)(2,1)S(1)}, u32[]{:S(2)}, u32[]{:S(2)}) async-start(bf16[16,8,16,256]{3,2,0,1:T(8,128)(2,1)} %copy.61), calls=%async_computation | async-start | bytes 2097152 | tf_op jit(solution)/shard_map/all_to_all | solution.py:51
  35.3 1.7 %copy-start.5 = (f32[256]{0:T(256)S(1)}, f32[256]{0:T(256)}, u32[]{:S(2)}) copy-start(f32[256]{0:T(256)} %param.11) | copy-start | bytes 3076
  51.6 3.0 %copy-start.1 = (bf16[16,128,256]{2,1,0:T(8,128)(2,1)S(1)}, bf16[16,128,256]{2,1,0:T(8,128)(2,1)}, u32[]{:S(2)}) copy-start(bf16[16,128,256]{2,1,0:T(8,128)(2,1)} %custom-call) | copy-start | bytes 3145732
  81.3 5.6 %copy-start.3 = (s32[32,4,16]{0,2,1:T(8,128)S(1)}, s32[32,4,16]{0,2,1:T(8,128)}, u32[]{:S(2)}) copy-start(s32[32,4,16]{0,2,1:T(8,128)} %param.17) | copy-start | bytes 24580
  81.3 5.7 %copy-start.4 = (s32[32,4,16]{0,2,1:T(8,128)S(1)}, s32[32,4,16]{0,2,1:T(8,128)}, u32[]{:S(2)}) copy-start(s32[32,4,16]{0,2,1:T(8,128)} %param.16) | copy-start | bytes 24580
  82.8 16.8 %all-to-all-start.1 = ((bf16[128,1,16,256]{3,2,1,0:T(8,128)(2,1)}), bf16[128,1,16,256]{3,2,1,0:T(8,128)(2,1)S(1)}, u32[]{:S(2)}, u32[]{:S(2)}) async-start(bf16[128,1,16,256]{3,2,1,0:T(8,128)(2,1)} %bitcast.79), calls=%async_computation.1 | async-start | bytes 2097152 | tf_op jit(solution)/shard_map/all_to_all | solution.py:68
  100.2 1.4 copy-start.6
where the time goes:
time: 153 us; the launch traced here: 152 us
  blocking collectives  42.4 us (28%)
  local copies, waits for them, and re-layouts  38.2 us (25%)
  waiting for transfers between devices  35.8 us (23%)
  matrix products  12.7 us (8%)
  starting transfers between devices  10.2 us (7%)
  other arithmetic  7 us (5%)
  between operations  5.09 us (3%)
    psum x1, blocking collectives, on_device(): loss_sum, mask_count = lax.psum((local_loss, local_count), ('seq', 'res'))  42.4 us
    all_to_all x1, waiting for transfers between devices, on_device(): lax.all_to_all(split_view, 'seq', split_axis=1, concat_axis=0, tiled=True)  23.3 us
    squeeze x16, local copies, waits for them, and re-layouts, on_device(): lax.map(per_column, projected).reshape(col_count * seq_total, features)  15.5 us
    all_to_all x1, waiting for transfers between devices, on_device(): lax.all_to_all(result, 'res', split_axis=0, concat_axis=1, tiled=True)  12.5 us
    convert_element_type x1, local copies, waits for them, and re-layouts, project(): return jnp.dot(normed, w_proj.reshape(features, 4 * features), preferred_...  6.52 us
    all_to_all x1, starting transfers between devices, on_device(): lax.all_to_all(split_view, 'seq', split_axis=1, concat_axis=0, tiled=True)  6.25 us
    dot_general x16, matrix products, column_attention(): jnp.einsum('shd,thd->hst', queries, key_part, preferred_element_type=jnp....  5.03 us
    unnamed x19, local copies, waits for them, and re-layouts  4.99 us
  transfers between devices with their start and end apart: 2, of which 2 were waited for; matrix products, arithmetic and copies ran while one was open for 0% of the time, Pallas kernels for 0%

commit v1 on v0

--- a/solution.py
+++ b/solution.py
@@ -5,6 +5,18 @@
 
 HEADS = 8
 HEAD_DIM = 32
+
+
+def _edit_squares(raw, dim_i, chunk):
+    q_next = raw.shape
+    mat_out = raw.reshape(*q_next[:dim_i], chunk, q_next[dim_i] // chunk, *q_next[dim_i + 1 :])
+    return jnp.moveaxis(mat_out, dim_i, 0)
+
+
+def reach_routes_all(mat, at_axis):
+    w_next = list(mat.shape[1:])
+    w_next[at_axis] *= mat.shape[0]
+    return jnp.moveaxis(mat, 0, at_axis).reshape(w_next)
 
 
 def normalize(values, gain):
@@ -48,7 +60,20 @@
     local_rows, single_block, segment, features = alignment.shape
     seq_devices = lax.axis_size("seq")
     split_view = alignment.reshape(local_rows, seq_devices, segment // seq_devices, features)
-    column_block = lax.all_to_all(split_view, "seq", split_axis=1, concat_axis=0, tiled=True)
+    top = lax.axis_size("seq")
+    kept_arr = lax.axis_index("seq")
+    field_out, carry_out = (top, kept_arr)
+    small = _edit_squares(split_view, 1, field_out)
+    block_list = [small[carry_out]]
+    kk = 1
+    while kk < field_out:
+        arr_out = small[carry_out ^ kk]
+        x_now = lax.ppermute(arr_out, axis_name="seq", perm=[(p, p ^ kk) for p in range(field_out)])
+        block_list.append(x_now)
+        kk = kk + 1
+    step_out = jnp.stack(block_list)
+    small = step_out[carry_out ^ jnp.arange(field_out)]
+    column_block = reach_routes_all(small, 0)
     seq_total, single, col_count, features = column_block.shape
     by_column = jnp.transpose(column_block.reshape(seq_total, col_count, features), (1, 0, 2))
     flat_rows = by_column.reshape(col_count * seq_total, features)

time: 153 us -> 152 us (level)
  the two profiles are of different devices: /device:TPU:12 before, /device:TPU:0 now
where the time goes in v1:
time: 152 us; the launch traced here: 151 us
  blocking collectives  43.6 us (29%)
  local copies, waits for them, and re-layouts  41.3 us (27%)
  waiting for transfers between devices  24.7 us (16%)
  starting transfers between devices  16.4 us (11%)
  matrix products  12 us (8%)
  other arithmetic  7.06 us (5%)
  between operations  5.3 us (3%)
    psum x1, blocking collectives, on_device(): loss_sum, mask_count = lax.psum((local_loss, local_count), ('seq', 'res'))  43.6 us
    squeeze x16, local copies, waits for them, and re-layouts, on_device(): lax.map(per_column, projected).reshape(col_count * seq_total, features)  15.5 us
    all_to_all x1, waiting for transfers between devices, on_device(): lax.all_to_all(result, 'res', split_axis=0, concat_axis=1, tiled=True)  13.3 us
    ppermute x7, starting transfers between devices, on_device(): lax.ppermute(arr_out, axis_name='seq', perm=[(p, p ^ kk) for p in range(f...  12.7 us
    ppermute x7, waiting for transfers between devices, on_device(): lax.ppermute(arr_out, axis_name='seq', perm=[(p, p ^ kk) for p in range(f...  11.4 us
    unnamed x30, local copies, waits for them, and re-layouts  8.42 us
    convert_element_type x1, local copies, waits for them, and re-layouts, project(): return jnp.dot(normed, w_proj.reshape(features, 4 * features), preferred_...  6.52 us
    dot_general x16, matrix products, column_attention(): jnp.einsum('shd,thd->hst', queries, key_part, preferred_element_type=jnp....  5.03 us
  transfers between devices with their start and end apart: 8, of which 2 were waited for; matrix products, arithmetic and copies ran while one was open for 3% of the time, Pallas kernels for 0%

profile of v1, /device:TPU:0, one launch (start us, length us, event | category | flops | bytes accessed | tf_op | source)
XLA Modules:
  0.0 151.1 jit_solution(11655106436328575513)
XLA Ops:
  0.7 1.4 dynamic-slice_bitcast_fusion.1
  2.1 3.0 %collective-permute-start = (bf16[16,1,16,256]{3,2,0,1:T(8,128)(2,1)S(1)}, bf16[16,1,16,256]{3,2,0,1:T(8,128)(2,1)}, u32[]{:S(2)}, u32[]{:S(2)}) collective-permute-start(bf16[16,1,16,256]{3,2,0,1:T(8,128)(2,1)S(1)} %get-tuple-element.68), channel_id=1, source_target_pairs={{0,4},{4,0},{8,12},{12,8},{16,20},{20,16},{24,28},{28,24},{1,5},{5... | collective-permute-start | bytes 393224 | tf_op jit(solution)/shard_map/ppermute | solution.py:71
  5.1 1.6 %collective-permute-start.1 = (bf16[16,1,16,256]{3,2,0,1:T(8,128)(2,1)S(1)}, bf16[16,1,16,256]{3,2,0,1:T(8,128)(2,1)}, u32[]{:S(2)}, u32[]{:S(2)}) collective-permute-start(bf16[16,1,16,256]{3,2,0,1:T(8,128)(2,1)S(1)} %get-tuple-element.67), channel_id=1, source_target_pairs={{0,8},{4,12},{8,0},{12,4},{16,24},{20,28},{24,16},{28,20},{1,9},{5... | collective-permute-start | bytes 393224 | tf_op jit(solution)/shard_map/ppermute | solution.py:71
  6.7 3.0 %collective-permute-start.3 = (bf16[16,1,16,256]{3,2,0,1:T(8,128)(2,1)S(1)}, bf16[16,1,16,256]{3,2,0,1:T(8,128)(2,1)S(1)}, u32[]{:S(2)}, u32[]{:S(2)}) collective-permute-start(bf16[16,1,16,256]{3,2,0,1:T(8,128)(2,1)S(1)} %get-tuple-element.65), channel_id=1, source_target_pairs={{0,16},{4,20},{8,24},{12,28},{16,0},{20,4},{24,8},{28,12},{1,17},{... | collective-permute-start | bytes 393224 | tf_op jit(solution)/shard_map/ppermute | solution.py:71
  9.7 1.3 collective-permute-start.4
  12.1 3.7 %collective-permute-start.5 = (bf16[16,1,16,256]{3,2,0,1:T(8,128)(2,1)S(1)}, bf16[16,1,16,256]{3,2,0,1:T(8,128)(2,1)S(1)}, u32[]{:S(2)}, u32[]{:S(2)}) collective-permute-start(bf16[16,1,16,256]{3,2,0,1:T(8,128)(2,1)S(1)} %get-tuple-element.63), channel_id=1, source_target_pairs={{0,24},{4,28},{8,16},{12,20},{16,8},{20,12},{24,0},{28,4},{1,25},{... | collective-permute-start | bytes 393224 | tf_op jit(solution)/shard_map/ppermute | solution.py:71
  17.8 11.4 %collective-permute-done.4 = bf16[16,1,16,256]{3,2,0,1:T(8,128)(2,1)S(1)} collective-permute-done((bf16[16,1,16,256]{3,2,0,1:T(8,128)(2,1)S(1)}, bf16[16,1,16,256]{3,2,0,1:T(8,128)(2,1)S(1)}, u32[]{:S(2)}, u32[]{:S(2)}) %collective-permute-start.4) | collective-permute-done | bytes 131104 | tf_op jit(solution)/shard_map/ppermute | solution.py:71
  30.2 1.2 bitcast_reduce_fusion
  31.3 1.2 copy.79
  32.6 1.6 %multiply_reduce_fusion.1 = f32[16,128]{1,0:T(8,128)S(1)} fusion(f32[16,128]{1,0:T(8,128)S(1)} %broadcast_multiply_fusion.1, f32[128,16,256]{2,1,0:T(8,128)S(1)} %bitcast_convert_fusion), kind=kLoop, calls=%fused_computation.25 | loop fusion | flops 1570816 | bytes 2113536 | tf_op jit(solution)/shard_map/reduce_sum | solution.py:25
  34.2 1.4 multiply_convert_fusion
  35.6 3.2 %convolution_convert_fusion = bf16[2048,1024]{1,0:T(8,128)(2,1)} fusion(bf16[2048,256]{1,0:T(8,128)(2,1)S(1)} %bitcast.151, bf16[256,1024]{1,0:T(8,128)(2,1)S(1)} %bitcast.153), kind=kOutput, calls=%fused_computation.13 | convolution fusion | flops 1075838976 | bytes 5767168 | tf_op jit(solution)/shard_map/dot_general | solution.py:32
  38.8 6.5 %copy.80 = bf16[2048,1024]{0,1:T(8,128)(2,1)} copy(bf16[2048,1024]{1,0:T(8,128)(2,1)} %convolution_convert_fusion) | data formatting | bytes 8388608 | tf_op jit(solution)/shard_map/convert_element_type | solution.py:34
  45.3 3.6 %copy.105 = bf16[128,8,16,128]{3,2,1,0:T(8,128)(2,1)S(1)} copy(bf16[128,8,16,128]{3,1,2,0:T(8,128)(2,1)} %bitcast.148) | data formatting | bytes 8388608
  48.9 3.0 %copy.81 = bf16[16,128,4,8,32]{1,4,3,2,0:T(8,128)(2,1)} copy(bf16[16,128,4,8,32]{1,0,4,3,2:T(8,128)(2,1)S(1)} %bitcast.149) | data formatting | bytes 8388608 | tf_op jit(solution)/shard_map/while | solution.py:90
  51.9 26.1 %while.10 = (s32[]{:T(128)}, bf16[16,128,256]{2,1,0:T(8,128)(2,1)S(1)}, bf16[16,128,4,8,32]{1,4,3,2,0:T(8,128)(2,1)}, s32[]{:T(128)}) while((s32[]{:T(128)}, bf16[16,128,256]{2,1,0:T(8,128)(2,1)S(1)}, bf16[16,128,4,8,32]{1,4,3,2,0:T(8,128)(2,1)}, s32[]{:T(128)}) %tuple.46), condition=%wide.region_4.0_spmd, body=%wide.region_2.4_spmd.sunk | while | flops 17398784 | bytes 1646653 | solution.py:90
  53.6 1.0 dynamic-slice_bitcast_fusion.9
  55.2 1.0 dynamic-slice_bitcast_fusion.9
  56.8 1.0 dynamic-slice_bitcast_fusion.9
  58.5 1.0 dynamic-slice_bitcast_fusion.9
  60.1 1.0 dynamic-slice_bitcast_fusion.9
  61.7 1.0 dynamic-slice_bitcast_fusion.9
  63.4 1.0 dynamic-slice_bitcast_fusion.9
  65.0 1.0 dynamic-slice_bitcast_fusion.9
  66.6 1.0 dynamic-slice_bitcast_fusion.9
  68.3 1.0 dynamic-slice_bitcast_fusion.9
  73.2 1.0 dynamic-slice_bitcast_fusion.9
  78.5 1.6 %copy.110 = bf16[16,128,256]{2,0,1:T(8,128)(2,1)} copy(bf16[16,128,256]{2,1,0:T(8,128)(2,1)S(1)} %bitcast.152) | data formatting | bytes 2097152 | tf_op jit(solution)/shard_map/reshape | solution.py:91
  80.1 3.7 %all-to-all-start = ((bf16[128,1,16,256]{3,2,1,0:T(8,128)(2,1)}), bf16[128,1,16,256]{3,2,1,0:T(8,128)(2,1)S(1)}, u32[]{:S(2)}, u32[]{:S(2)}) async-start(bf16[128,1,16,256]{3,2,1,0:T(8,128)(2,1)} %bitcast.125), calls=%async_computation | async-start | bytes 2097152 | tf_op jit(solution)/shard_map/all_to_all | solution.py:93
  84.7 13.3 %all-to-all-done = bf16[128,1,16,256]{3,2,1,0:T(8,128)(2,1)S(1)} async-done(((bf16[128,1,16,256]{3,2,1,0:T(8,128)(2,1)}), bf16[128,1,16,256]{3,2,1,0:T(8,128)(2,1)S(1)}, u32[]{:S(2)}, u32[]{:S(2)}) %all-to-all-start) | async-done | bytes 1048608 | tf_op jit(solution)/shard_map/all_to_all | solution.py:93
  102.1 43.6 %all-reduce = (f32[]{:T(128)}, f32[]{:T(128)}) all-reduce(f32[]{:T(128)} %get-tuple-element.51, f32[]{:T(128)} %get-tuple-element.50), channel_id=1, replica_groups=mesh['seq'=8,'res'=4] {'seq','res'}, use_global_device_ids=true, to_apply=%region_10.11 | all-reduce | flops 2 | bytes 16 | tf_op jit(solution)/shard_map/psum | solution.py:103
  147.0 1.1 copy.92
  (132 shorter events, 24.1 us)
Async XLA Ops:
  0.6 77.4 %copy-start = (bf16[256,256]{1,0:T(8,128)(2,1)S(1)}, bf16[256,256]{1,0:T(8,128)(2,1)}, u32[]{:S(2)}) copy-start(bf16[256,256]{1,0:T(8,128)(2,1)} %param.13) | copy-start | bytes 393220
  0.6 10.4 %copy-start.2 = (bf16[256,4,256]{2,1,0:T(4,128)(2,1)S(1)}, bf16[256,4,256]{2,1,0:T(4,128)(2,1)}, u32[]{:S(2)}) copy-start(bf16[256,4,256]{2,1,0:T(4,128)(2,1)} %param.12) | copy-start | bytes 1572868
  2.1 9.9 %collective-permute-start = (bf16[16,1,16,256]{3,2,0,1:T(8,128)(2,1)S(1)}, bf16[16,1,16,256]{3,2,0,1:T(8,128)(2,1)}, u32[]{:S(2)}, u32[]{:S(2)}) collective-permute-start(bf16[16,1,16,256]{3,2,0,1:T(8,128)(2,1)S(1)} %get-tuple-element.68), channel_id=1, source_target_pairs={{0,4},{4,0},{8,12},{12,8},{16,20},{20,16},{24,28},{28,24},{1,5},{5... | collective-permute-start | bytes 393224 | tf_op jit(solution)/shard_map/ppermute | solution.py:71
  5.1 11.5 %collective-permute-start.1 = (bf16[16,1,16,256]{3,2,0,1:T(8,128)(2,1)S(1)}, bf16[16,1,16,256]{3,2,0,1:T(8,128)(2,1)}, u32[]{:S(2)}, u32[]{:S(2)}) collective-permute-start(bf16[16,1,16,256]{3,2,0,1:T(8,128)(2,1)S(1)} %get-tuple-element.67), channel_id=1, source_target_pairs={{0,8},{4,12},{8,0},{12,4},{16,24},{20,28},{24,16},{28,20},{1,9},{5... | collective-permute-start | bytes 393224 | tf_op jit(solution)/shard_map/ppermute | solution.py:71
  6.7 11.0 %collective-permute-start.2 = (bf16[16,1,16,256]{3,2,0,1:T(8,128)(2,1)S(1)}, bf16[16,1,16,256]{3,2,0,1:T(8,128)(2,1)S(1)}, u32[]{:S(2)}, u32[]{:S(2)}) collective-permute-start(bf16[16,1,16,256]{3,2,0,1:T(8,128)(2,1)S(1)} %get-tuple-element.66), channel_id=1, source_target_pairs={{0,12},{4,8},{8,4},{12,0},{16,28},{20,24},{24,20},{28,16},{1,13},{... | collective-permute-start | bytes 393224 | tf_op jit(solution)/shard_map/ppermute | solution.py:71
  6.7 11.0 %collective-permute-start.3 = (bf16[16,1,16,256]{3,2,0,1:T(8,128)(2,1)S(1)}, bf16[16,1,16,256]{3,2,0,1:T(8,128)(2,1)S(1)}, u32[]{:S(2)}, u32[]{:S(2)}) collective-permute-start(bf16[16,1,16,256]{3,2,0,1:T(8,128)(2,1)S(1)} %get-tuple-element.65), channel_id=1, source_target_pairs={{0,16},{4,20},{8,24},{12,28},{16,0},{20,4},{24,8},{28,12},{1,17},{... | collective-permute-start | bytes 393224 | tf_op jit(solution)/shard_map/ppermute | solution.py:71
  9.7 19.4 %collective-permute-start.4 = (bf16[16,1,16,256]{3,2,0,1:T(8,128)(2,1)S(1)}, bf16[16,1,16,256]{3,2,0,1:T(8,128)(2,1)S(1)}, u32[]{:S(2)}, u32[]{:S(2)}) collective-permute-start(bf16[16,1,16,256]{3,2,0,1:T(8,128)(2,1)S(1)} %get-tuple-element.64), channel_id=1, source_target_pairs={{0,20},{4,16},{8,28},{12,24},{16,4},{20,0},{24,12},{28,8},{1,21},{... | collective-permute-start | bytes 393224 | tf_op jit(solution)/shard_map/ppermute | solution.py:71
  12.1 17.1 %collective-permute-start.5 = (bf16[16,1,16,256]{3,2,0,1:T(8,128)(2,1)S(1)}, bf16[16,1,16,256]{3,2,0,1:T(8,128)(2,1)S(1)}, u32[]{:S(2)}, u32[]{:S(2)}) collective-permute-start(bf16[16,1,16,256]{3,2,0,1:T(8,128)(2,1)S(1)} %get-tuple-element.63), channel_id=1, source_target_pairs={{0,24},{4,28},{8,16},{12,20},{16,8},{20,12},{24,0},{28,4},{1,25},{... | collective-permute-start | bytes 393224 | tf_op jit(solution)/shard_map/ppermute | solution.py:71
  16.7 12.5 %collective-permute-start.6 = (bf16[16,1,16,256]{3,2,0,1:T(8,128)(2,1)S(1)}, bf16[16,1,16,256]{3,2,0,1:T(8,128)(2,1)S(1)}, u32[]{:S(2)}, u32[]{:S(2)}) collective-permute-start(bf16[16,1,16,256]{3,2,0,1:T(8,128)(2,1)S(1)} %get-tuple-element.62), channel_id=1, source_target_pairs={{0,28},{4,24},{8,20},{12,16},{16,12},{20,8},{24,4},{28,0},{1,29},{... | collective-permute-start | bytes 393224 | tf_op jit(solution)/shard_map/ppermute | solution.py:71
  32.6 1.7 %copy-start.7 = (f32[256]{0:T(256)S(1)}, f32[256]{0:T(256)}, u32[]{:S(2)}) copy-start(f32[256]{0:T(256)} %param.11) | copy-start | bytes 3076
  48.9 3.0 %copy-start.1 = (bf16[16,128,256]{2,1,0:T(8,128)(2,1)S(1)}, bf16[16,128,256]{2,1,0:T(8,128)(2,1)}, u32[]{:S(2)}) copy-start(bf16[16,128,256]{2,1,0:T(8,128)(2,1)} %custom-call.3) | copy-start | bytes 3145732
  78.5 5.3 %copy-start.4 = (s32[32,4,16]{0,2,1:T(8,128)S(1)}, s32[32,4,16]{0,2,1:T(8,128)}, u32[]{:S(2)}) copy-start(s32[32,4,16]{0,2,1:T(8,128)} %param.17) | copy-start | bytes 24580
  78.5 5.5 %copy-start.5 = (s32[32,4,16]{0,2,1:T(8,128)S(1)}, s32[32,4,16]{0,2,1:T(8,128)}, u32[]{:S(2)}) copy-start(s32[32,4,16]{0,2,1:T(8,128)} %param.16) | copy-start | bytes 24580
  80.1 17.9 %all-to-all-start = ((bf16[128,1,16,256]{3,2,1,0:T(8,128)(2,1)}), bf16[128,1,16,256]{3,2,1,0:T(8,128)(2,1)S(1)}, u32[]{:S(2)}, u32[]{:S(2)}) async-start(bf16[128,1,16,256]{3,2,1,0:T(8,128)(2,1)} %bitcast.125), calls=%async_computation | async-start | bytes 2097152 | tf_op jit(solution)/shard_map/all_to_all | solution.py:93
  98.4 1.6 %copy-start.8 = (f32[256]{0:T(256)S(1)}, f32[256]{0:T(256)}, u32[]{:S(2)}) copy-start(f32[256]{0:T(256)} %param.14) | copy-start | bytes 3076
  99.0 2.0 %copy-start.6 = (bf16[256,23]{0,1:T(8,128)(2,1)S(1)}, bf16[256,23]{0,1:T(8,128)(2,1)}, u32[]{:S(2)}) copy-start(bf16[256,23]{0,1:T(8,128)(2,1)} %param.15) | copy-start | bytes 35332
  100.0 1.4 copy-start.3
